TPU v7x, 32 devices: a whole 2x2x4 slice. The times are simulated.
32 devices in a mesh: ep: 4 (over y, x), grp: 8 (over z, core).
Axes of the slice: x: 2, y: 2, z: 4, core: 2. Of those that a mesh axis runs over, the one named last changes fastest.
Arguments:
- tokens: bfloat16 [4096, 4096], P(('ep', 'grp')), may hold values from -6 to 6
- expert_ids: int32 [4096, 8], P(('ep', 'grp')), may hold values from 0 to 127, all different within a row; in each aligned block of 128 rows (0 to 127, 128 to 255, ...) at most 16 rows name the same one
- combine: float32 [4096, 8], P(('ep', 'grp')), may hold values from 0.05 to 1
- w_gate: bfloat16 [4096, 1280], P(None, 'ep'), may hold values from -0.09375 to 0.09375
- w_up: bfloat16 [4096, 1280], P(None, 'ep'), may hold values from -0.09375 to 0.09375
- w_down: bfloat16 [1280, 4096], P('ep'), may hold values from -0.15625 to 0.15625
- bias: float32 [128], replicated, may hold values from -3 to 3
Outputs:
- mixed: bfloat16 [4096, 4096], P(('ep', 'grp'))
- new_bias: float32 [128], replicated
Inputs may be any that keep to these rules, and one draw needn't show every extreme that they name: `expert_ids`: each row names 8 different experts. Among the rows of one device no expert is named more than 16 times, a bound that some block reaches.
All inputs are finite; a program needn't handle non-finite values.
Results may differ from a plain program's by a relative error of at most 0.0057.
Values may be sent and summed in bfloat16 or wider, within the bound.
A program may use at most 64 MiB of HBM per device.

v0:
```python
import jax
import jax.numpy as jnp
from jax import lax
from jax.sharding import PartitionSpec as P

NEXP = 128
TOPK = 8
SPLIT = 4


def count_loads(expert_ids):
    experts = jnp.arange(NEXP, dtype=jnp.int32)
    local = jnp.sum(
        (expert_ids.reshape(-1)[:, None] == experts[None, :]).astype(jnp.float32), axis=0
    )
    within = lax.psum(local, "ep")
    return lax.psum(within, "grp")


def per_device(tokens, expert_ids, combine, w_gate, w_up, w_down, bias):
    n_ep = lax.axis_size("ep")
    n_grp = lax.axis_size("grp")
    tok_rows = tokens.shape[0]
    width = tokens.shape[1]
    capacity = tok_rows // 8
    win_experts = n_ep // SPLIT
    flat_ids = expert_ids.reshape(-1)
    window = jnp.arange(win_experts, dtype=jnp.int32)
    hit = (flat_ids[:, None] == window[None, :]).astype(jnp.int32)
    ranks = jnp.cumsum(hit, axis=0) - 1
    slot = jnp.sum(hit * ranks, axis=1)
    inside = jnp.sum(hit, axis=1)
    dest = jnp.where(inside > 0, flat_ids * capacity + slot, win_experts * capacity)
    slot_ids = jnp.arange(win_experts * capacity, dtype=jnp.int32)
    chosen = (slot_ids[:, None] == dest[None, :]).reshape(win_experts * capacity, tok_rows, TOPK)
    select = jnp.sum(chosen.astype(jnp.float32), axis=2)
    weights = jnp.sum(chosen.astype(jnp.float32) * combine[None, :, :], axis=2)
    buffer = jnp.dot(
        select.astype(jnp.bfloat16), tokens, preferred_element_type=jnp.float32
    ).astype(jnp.bfloat16)
    outgoing = jnp.repeat(buffer.reshape(win_experts, capacity, width), SPLIT, axis=0)
    block = lax.all_to_all(outgoing, "ep", split_axis=0, concat_axis=0, tiled=True)
    rows = block.reshape(-1, width)
    gate = jnp.dot(rows, w_gate, preferred_element_type=jnp.float32)
    upval = jnp.dot(rows, w_up, preferred_element_type=jnp.float32)
    hidden = (jax.nn.silu(gate) * upval).astype(jnp.bfloat16)
    part = jnp.dot(hidden, w_down, preferred_element_type=jnp.float32).astype(jnp.bfloat16)
    returned = lax.all_to_all(
        part.reshape(block.shape), "ep", split_axis=0, concat_axis=0, tiled=True
    )
    summed = jnp.sum(
        returned.astype(jnp.float32).reshape(win_experts, SPLIT, capacity, width), axis=1
    )
    summed = summed.reshape(win_experts * capacity, width)
    mixed = jnp.dot(
        weights.T, summed, precision=lax.Precision.HIGHEST, preferred_element_type=jnp.float32
    ).astype(jnp.bfloat16)
    load = count_loads(expert_ids)
    mean_load = jnp.float32(tok_rows * n_ep * n_grp * TOPK / NEXP)
    new_bias = bias - 0.05 * (load - mean_load) / jnp.sqrt(mean_load)
    return (mixed, new_bias)


def solution(mesh):
    return jax.shard_map(
        per_device,
        mesh=mesh,
        in_specs=(
            P(("ep", "grp"), None),
            P(("ep", "grp"), None),
            P(("ep", "grp"), None),
            P(None, "ep"),
            P(None, "ep"),
            P("ep", None),
            P(),
        ),
        out_specs=(P(("ep", "grp"), None), P()),
        check_vma=False,
    )
```

profile of v0, /device:TPU:0, one launch (start us, length us, event | category | flops | bytes accessed | tf_op | source)
XLA Modules:
  0.0 56.3 jit_solution(11772067957491407302)
XLA Ops:
  0.6 0.8 %fusion.8 = s32[128,8]{0,1:T(8,128)S(1)} fusion(s32[128,8]{0,1:T(8,128)} %param.8), kind=kLoop, calls=%fused_computation.21 | loop fusion | flops 2048 | bytes 8192 | tf_op jit(solution)/shard_map/convert_element_type | solution.py:29
  1.5 0.1 copy.30
  1.6 0.1 reshape.124
  1.7 0.3 reduce-window.6
  2.0 0.2 slice_reduce_fusion
  2.2 0.1 reshape.117
  2.2 0.2 reduce-window.9
  2.4 0.1 broadcast.76
  2.5 0.1 reshape.120
  2.7 0.9 %add_select_fusion = s32[128,8]{0,1:T(8,128)S(1)} fusion(s32[128,8]{0,1:T(8,128)S(1)} %copy.31, s32[128,8]{0,1:T(8,128)S(1)} %copy.32, s32[128,8]{0,1:T(8,128)} %param.8), kind=kLoop, calls=%fused_computation.18 | loop fusion | flops 9216 | bytes 16384 | tf_op jit(solution)/shard_map/jit(_where)/select_n | solution.py:33
  3.6 0.7 %convert_reduce_fusion.2 = (bf16[16,128]{1,0:T(8,128)(2,1)S(1)}, f32[16,128]{1,0:T(8,128)S(1)}) fusion(s32[128,8]{0,1:T(8,128)S(1)} %add_select_fusion, f32[128,8]{0,1:T(8,128)} %param.9), kind=kLoop, calls=%fused_computation.13 | loop fusion | flops 77824 | bytes 20480 | tf_op jit(solution)/shard_map/reduce_sum | solution.py:36
  4.3 1.5 %convolution_convert_fusion.2 = bf16[16,4096]{1,0:T(8,128)(2,1)S(1)} fusion(bf16[128,4096]{1,0:T(8,128)(2,1)} %param.7, bf16[16,128]{1,0:T(8,128)(2,1)S(1)} %get-tuple-element.2), kind=kOutput, calls=%fused_computation.2 | convolution fusion | flops 16842752 | bytes 1183744 | tf_op jit(solution)/shard_map/dot_general | solution.py:38
  5.8 13.5 %all_to_all.10 = bf16[4,16,4096]{2,1,0:T(8,128)(2,1)S(1)} all-to-all(bf16[4,16,4096]{2,1,0:T(8,128)(2,1)S(1)} %reshape.121), channel_id=1, replica_groups=mesh['ep'=4,'grp'=8] {'ep'}, dimensions={0} | all-to-all | bytes 1048576 | tf_op jit(solution)/shard_map/all_to_all | solution.py:42
  19.3 0.9 %fusion.10 = f32[64,320]{1,0:T(8,128)S(1)} fusion(bf16[64,4096]{1,0:T(8,128)(2,1)S(1)} %bitcast.16, bf16[4096,320]{0,1:T(8,128)(2,1)S(1)} %copy-done.1), kind=kOutput, calls=%fused_computation.25 | convolution fusion | flops 167772160 | bytes 3227648 | tf_op jit(solution)/shard_map/dot_general | solution.py:44
  20.3 4.7 %convolution_convert_fusion.1 = bf16[64,4096]{1,0:T(8,128)(2,1)} fusion(bf16[320,4096]{1,0:T(8,128)(2,1)S(1)} %copy-done, bf16[64,4096]{1,0:T(8,128)(2,1)S(1)} %bitcast.17, bf16[4096,320]{0,1:T(8,128)(2,1)} %param.11, f32[64,320]{1,0:T(8,128)S(1)} %fusion.10), kind=kOutput, calls=%fused_computation.1 | convolution fusion | flops 335929344 | bytes 6373376 | tf_op jit(solution)/shard_map/dot_general | solution.py:47
  25.0 3.5 %all-to-all-start.1 = ((bf16[4,16,4096]{2,1,0:T(8,128)(2,1)}), bf16[4,16,4096]{2,1,0:T(8,128)(2,1)S(1)}, u32[]{:S(2)}, u32[]{:S(2)}) async-start(bf16[4,16,4096]{2,1,0:T(8,128)(2,1)} %bitcast.18), calls=%async_computation.1 | async-start | bytes 1048576 | tf_op jit(solution)/shard_map/all_to_all | solution.py:48
  28.5 0.1 copy.33
  28.6 0.1 eq.58
  28.7 0.2 convert_reduce_fusion.1
  28.9 10.4 %psum.14 = f32[128]{0:T(128)S(1)} all-reduce(f32[128]{0:T(128)S(1)} %convert_reduce_fusion.1), channel_id=1, replica_groups=mesh['ep'=4,'grp'=8] {'ep'}, use_global_device_ids=true, to_apply=%region_6.7 | all-reduce | flops 128 | bytes 1024 | tf_op jit(solution)/shard_map/psum | solution.py:16
  39.3 13.6 %psum.15 = f32[128]{0:T(128)S(1)} all-reduce(f32[128]{0:T(128)S(1)} %psum.14), channel_id=1, replica_groups=mesh['ep'=4,'grp'=8] {'grp'}, use_global_device_ids=true, to_apply=%region_7.8 | all-reduce | flops 128 | bytes 1024 | tf_op jit(solution)/shard_map/psum | solution.py:17
  52.9 0.5 multiply_subtract_fusion
  53.4 0.1 convert_reduce_fusion
  53.5 2.8 %convolution_convert_fusion = bf16[128,4096]{1,0:T(8,128)(2,1)} fusion(f32[16,128]{1,0:T(8,128)S(1)} %get-tuple-element.3, f32[16,4096]{1,0:T(8,128)S(1)} %convert_reduce_fusion), kind=kOutput, calls=%fused_computation | convolution fusion | flops 101187584 | bytes 1318912 | tf_op jit(solution)/shard_map/dot_general | solution.py:55
  (13 shorter events, 0.2 us)
Async XLA Ops:
  0.6 19.6 %copy-start = (bf16[320,4096]{1,0:T(8,128)(2,1)S(1)}, bf16[320,4096]{1,0:T(8,128)(2,1)}, u32[]{:S(2)}) copy-start(bf16[320,4096]{1,0:T(8,128)(2,1)} %param.12) | copy-start | bytes 7864324
  2.7 16.6 %copy-start.1 = (bf16[4096,320]{0,1:T(8,128)(2,1)S(1)}, bf16[4096,320]{0,1:T(8,128)(2,1)}, u32[]{:S(2)}) copy-start(bf16[4096,320]{0,1:T(8,128)(2,1)} %param.10) | copy-start | bytes 7864324
  20.2 8.2 %copy-start.2 = (s32[128,8]{0,1:T(8,128)S(1)}, s32[128,8]{0,1:T(8,128)}, u32[]{:S(2)}) copy-start(s32[128,8]{0,1:T(8,128)} %param.8) | copy-start | bytes 12292
  20.3 32.6 %copy-start.3 = (f32[128]{0:T(128)S(1)}, f32[128]{0:T(128)}, u32[]{:S(2)}) copy-start(f32[128]{0:T(128)} %param.13) | copy-start | bytes 1540
  25.0 28.4 %all-to-all-start.1 = ((bf16[4,16,4096]{2,1,0:T(8,128)(2,1)}), bf16[4,16,4096]{2,1,0:T(8,128)(2,1)S(1)}, u32[]{:S(2)}, u32[]{:S(2)}) async-start(bf16[4,16,4096]{2,1,0:T(8,128)(2,1)} %bitcast.18), calls=%async_computation.1 | async-start | bytes 1048576 | tf_op jit(solution)/shard_map/all_to_all | solution.py:48
where the time goes:
time: 56.6 us; the launch traced here: 56.3 us
  blocking collectives  37.5 us (66%)
  matrix products  9.9 us (17%)
  other arithmetic  3.71 us (7%)
  starting transfers between devices  3.47 us (6%)
  local copies, waits for them, and re-layouts  1 us (2%)
  between operations  0.72 us (1%)
    psum x1, blocking collectives, count_loads(): return lax.psum(within, 'grp')  13.6 us
    all_to_all x1, blocking collectives, per_device(): lax.all_to_all(outgoing, 'ep', split_axis=0, concat_axis=0, tiled=True)  13.5 us
    psum x1, blocking collectives, count_loads(): within = lax.psum(local, 'ep')  10.4 us
    dot_general x1, matrix products, per_device(): jnp.dot(hidden, w_down, preferred_element_type=jnp.float32)  4.74 us
    all_to_all x1, starting transfers between devices, per_device(): lax.all_to_all(part.reshape(block.shape), 'ep', split_axis=0, concat_axis...  3.47 us
    dot_general x1, matrix products, per_device(): jnp.dot(weights.T, summed, precision=lax.Precision.HIGHEST, preferred_ele...  2.81 us
    dot_general x1, matrix products, per_device(): jnp.dot(select.astype(jnp.bfloat16), tokens, preferred_element_type=jnp.f...  1.47 us
  transfers between devices with their start and end apart: 1, of which 0 were waited for; matrix products, arithmetic and copies ran while one was open for 2% of the time, Pallas kernels for 0%

commit v1 on v0

v1 whole, which is shorter than its diff:
```python
import functools

import jax
import jax.numpy as jnp
from jax import lax
from jax.experimental import pallas as pl
from jax.experimental.pallas import tpu as pltpu
from jax.sharding import PartitionSpec as P

SPLIT = 4
MESH = pl.DeviceIdType.MESH
ANY = pl.BlockSpec(memory_space=pl.ANY)
VMEM = pl.BlockSpec(memory_space=pltpu.VMEM)
F32 = jnp.float32
BF16 = jnp.bfloat16
IN_CHUNKS = 4
OUT_CHUNKS = 4
NT = (((1,), (1,)), ((), ()))
TN = (((0,), (0,)), ((), ()))


def partner(me, n, d):
    blocks = n // 4
    x, y, block = me % 2, (me // 2) % 2, me // 4
    return ((block + d // 4) % blocks) * 4 + ((y + (d % 4) // 2) % 2) * 2 + (x + d % 2) % 2


def exchange(
    n_ep, n_grp, n_exp, cap,
    tok_hbm, ids_hbm, comb_hbm, wg_hbm, wu_hbm, wd_hbm,
    scaled_ref, sel_ref, load_ref,
    tok, ids, comb, w_in, w_out, buf, rows, part, back, acc, load_ep, load_grp,
    loc_sem, send_in, recv_in, send_out, recv_out, load_send, load_recv,
):
    win = n_ep // SPLIT
    tokens, width = tok.shape
    ff = w_out.shape[0]
    kc, nc = width // IN_CHUNKS, width // OUT_CHUNKS
    me, grp = lax.axis_index("ep"), lax.axis_index("grp")
    order = sorted(range(1, n_ep), key=lambda d: -(d % 4 == 3))

    barrier = pltpu.get_barrier_semaphore()
    for d in range(1, n_ep):
        pl.semaphore_signal(barrier, inc=1, device_id=(partner(me, n_ep, d), grp), device_id_type=MESH)
    for d in range(1, n_grp):
        pl.semaphore_signal(barrier, inc=1, device_id=(me, (grp + d) % n_grp), device_id_type=MESH)

    sem = iter(range(loc_sem.shape[0]))

    def load(src, dst):
        copy = pltpu.make_async_copy(src, dst, loc_sem.at[next(sem)])
        copy.start()
        return copy

    get_ids = load(ids_hbm, ids)
    get_comb = load(comb_hbm, comb)
    get_tok = [load(tok_hbm.at[:, pl.ds(c * kc, kc)], tok.at[:, pl.ds(c * kc, kc)]) for c in range(IN_CHUNKS)]
    get_in = []
    for c in range(IN_CHUNKS):
        cols = pl.ds(c * kc, kc)
        get_in.append((load(wg_hbm.at[:, cols], w_in.at[pl.ds(0, ff), cols]),
                       load(wu_hbm.at[:, cols], w_in.at[pl.ds(ff, ff), cols])))
    get_out = [load(wd_hbm.at[:, pl.ds(c * nc, nc)], w_out.at[:, pl.ds(c * nc, nc)]) for c in range(OUT_CHUNKS)]

    get_ids.wait()
    top = ids.shape[0]
    names = lax.broadcasted_iota(jnp.int32, (n_exp, tokens), 0)
    hits = jnp.zeros((n_exp, tokens), F32)
    for p in range(top):
        hits += (names == ids[p:p + 1, :]).astype(F32)
    head = -(-win // 8) * 8
    earlier = (lax.broadcasted_iota(jnp.int32, (tokens, tokens), 0)
               < lax.broadcasted_iota(jnp.int32, (tokens, tokens), 1)).astype(F32).astype(BF16)
    rank = jnp.dot(hits[:head].astype(BF16), earlier, preferred_element_type=F32)
    places = lax.broadcasted_iota(jnp.int32, (cap, tokens), 0).astype(F32)
    picked = [jnp.where(rank[w:w + 1] == places, 1.0, 0.0) * hits[w:w + 1] for w in range(win)]
    select = jnp.concatenate(picked, axis=0) if win > 1 else picked[0]
    select_b = select.astype(BF16)

    sends_in = []
    for c in range(IN_CHUNKS):
        cols = pl.ds(c * kc, kc)
        get_tok[c].wait()
        buf[:, :, cols] = jnp.dot(select_b, tok[:, cols], preferred_element_type=F32).astype(BF16).reshape(win, cap, kc)
        if c == 0:
            pl.semaphore_wait(barrier, n_ep + n_grp - 2)
        row = []
        for d in order:
            to = partner(me, n_ep, d)
            copy = pltpu.make_async_remote_copy(
                src_ref=buf.at[to // SPLIT, :, cols], dst_ref=rows.at[me, :, cols],
                send_sem=send_in.at[c, d], recv_sem=recv_in.at[c, d],
                device_id=(to, grp), device_id_type=MESH)
            copy.start()
            row.append(copy)
        rows[me, :, cols] = buf[me // SPLIT, :, cols]
        sends_in.append(row)

    ones = jnp.ones((8, tokens), BF16)
    load_ep[me] = lax.dot_general(ones, hits.astype(BF16), NT, preferred_element_type=F32)
    sends_load = []
    for d in range(1, n_ep):
        copy = pltpu.make_async_remote_copy(
            src_ref=load_ep.at[me], dst_ref=load_ep.at[me], send_sem=load_send.at[d], recv_sem=load_recv.at[d],
            device_id=(partner(me, n_ep, d), grp), device_id_type=MESH)
        copy.start()
        sends_load.append(copy)
    sel_ref[...] = jnp.concatenate([select_b, select_b], axis=0)
    get_comb.wait()
    weights = []
    for w in range(win):
        named = jnp.sum(jnp.where(ids[...] == w, comb[...], 0.0), axis=0, keepdims=True)
        weights.append(jnp.sum(picked[w] * named, axis=1, keepdims=True))
    weight = jnp.concatenate(weights, axis=0) if win > 1 else weights[0]

    for c in range(IN_CHUNKS):
        cols = pl.ds(c * kc, kc)
        for copy in get_in[c]:
            copy.wait()
        for copy in sends_in[c]:
            copy.wait_recv()
        x = rows[:, :, cols].reshape(n_ep * cap, kc)
        term = lax.dot_general(x, w_in[:, cols], NT, preferred_element_type=F32)
        acc[...] = term if c == 0 else acc[...] + term

    gate, up = acc[:, :ff], acc[:, ff:]
    hidden = (jax.nn.silu(gate) * up).astype(BF16)

    sends_out = []
    for c in range(OUT_CHUNKS):
        cols = pl.ds(c * nc, nc)
        get_out[c].wait()
        value = jnp.dot(hidden, w_out[:, cols], preferred_element_type=F32)
        part[:, :, cols] = value.astype(BF16).reshape(n_ep, cap, nc)
        row = []
        for d in order:
            to = partner(me, n_ep, d)
            copy = pltpu.make_async_remote_copy(
                src_ref=part.at[to, :, cols], dst_ref=back.at[me, :, cols],
                send_sem=send_out.at[c, d], recv_sem=recv_out.at[c, d],
                device_id=(to, grp), device_id_type=MESH)
            copy.start()
            row.append(copy)
        back[me, :, cols] = part[me, :, cols]
        sends_out.append(row)
        if c == 0:
            for copy in sends_load:
                copy.wait_recv()
            load_grp[grp] = jnp.sum(load_ep[...], axis=0)
            sends_grp = []
            for d in range(1, n_grp):
                copy = pltpu.make_async_remote_copy(
                    src_ref=load_grp.at[grp], dst_ref=load_grp.at[grp],
                    send_sem=load_send.at[n_ep + d], recv_sem=load_recv.at[n_ep + d],
                    device_id=(me, (grp + d) % n_grp), device_id_type=MESH)
                copy.start()
                sends_grp.append(copy)

    for c in range(OUT_CHUNKS):
        cols = pl.ds(c * nc, nc)
        for copy in sends_out[c]:
            copy.wait_recv()
        total = jnp.sum(back[:, :, cols].astype(F32).reshape(win, SPLIT, cap, nc), axis=1).reshape(win * cap, nc)
        scaled = total * weight
        high = scaled.astype(BF16)
        scaled_ref[:win * cap, cols] = high
        scaled_ref[win * cap:, cols] = (scaled - high.astype(F32)).astype(BF16)
        if c == 0:
            for copy in sends_grp:
                copy.wait_recv()
            load_ref[...] = jnp.sum(load_grp[...], axis=0)

    for row in sends_in + sends_out + [sends_load, sends_grp]:
        for copy in row:
            copy.wait_send()


def finish(mean, scaled_ref, sel_ref, load_ref, bias_ref, mixed_ref, new_ref):
    mixed_ref[...] = lax.dot_general(sel_ref[...], scaled_ref[...], TN, preferred_element_type=F32).astype(BF16)
    new_ref[...] = bias_ref[...] - 0.05 * (load_ref[:1, :] - mean) / jnp.sqrt(jnp.full((1, 1), mean, F32))


def per_device(n_ep, n_grp, tokens, expert_ids, combine, w_gate, w_up, w_down, bias):
    rows, width = tokens.shape
    top = expert_ids.shape[1]
    n_exp = bias.shape[0]
    ff = w_down.shape[0]
    cap = rows // 8
    slots = (n_ep // SPLIT) * cap
    mean = float(rows * n_ep * n_grp * top / n_exp)
    scaled, sel, load = pl.pallas_call(
        functools.partial(exchange, n_ep, n_grp, n_exp, cap),
        out_shape=(
            jax.ShapeDtypeStruct((2 * slots, width), BF16),
            jax.ShapeDtypeStruct((2 * slots, rows), BF16),
            jax.ShapeDtypeStruct((8, n_exp), F32),
        ),
        in_specs=[ANY] * 6,
        out_specs=(VMEM, VMEM, VMEM),
        scratch_shapes=[
            pltpu.VMEM((rows, width), BF16),
            pltpu.VMEM((top, rows), jnp.int32),
            pltpu.VMEM((top, rows), F32),
            pltpu.VMEM((2 * ff, width), BF16),
            pltpu.VMEM((ff, width), BF16),
            pltpu.VMEM((n_ep // SPLIT, cap, width), BF16),
            pltpu.VMEM((n_ep, cap, width), BF16),
            pltpu.VMEM((n_ep, cap, width), BF16),
            pltpu.VMEM((n_ep, cap, width), BF16),
            pltpu.VMEM((n_ep * cap, 2 * ff), F32),
            pltpu.VMEM((n_ep, 8, n_exp), F32),
            pltpu.VMEM((n_grp, 8, n_exp), F32),
            pltpu.SemaphoreType.DMA((2 + 3 * IN_CHUNKS + OUT_CHUNKS,)),
            pltpu.SemaphoreType.DMA((IN_CHUNKS, n_ep)),
            pltpu.SemaphoreType.DMA((IN_CHUNKS, n_ep)),
            pltpu.SemaphoreType.DMA((OUT_CHUNKS, n_ep)),
            pltpu.SemaphoreType.DMA((OUT_CHUNKS, n_ep)),
            pltpu.SemaphoreType.DMA((n_ep + n_grp,)),
            pltpu.SemaphoreType.DMA((n_ep + n_grp,)),
        ],
        compiler_params=pltpu.CompilerParams(
            collective_id=0, has_side_effects=True, vmem_limit_bytes=40 * 1024 * 1024),
        name="exchange",
    )(tokens, expert_ids.T, combine.T, w_gate.T, w_up.T, w_down)
    steps = 4
    tile = width // steps
    mixed, new_bias = pl.pallas_call(
        functools.partial(finish, mean),
        grid=(steps,),
        out_shape=(jax.ShapeDtypeStruct((rows, width), BF16), jax.ShapeDtypeStruct((1, n_exp), F32)),
        in_specs=[
            pl.BlockSpec((2 * slots, tile), lambda i: (0, i)),
            pl.BlockSpec((2 * slots, rows), lambda i: (0, 0)),
            pl.BlockSpec((8, n_exp), lambda i: (0, 0)),
            pl.BlockSpec((1, n_exp), lambda i: (0, 0)),
        ],
        out_specs=(pl.BlockSpec((rows, tile), lambda i: (0, i)), pl.BlockSpec((1, n_exp), lambda i: (0, 0))),
        name="finish",
    )(scaled, sel, load, bias.reshape(1, n_exp))
    return mixed, new_bias.reshape(n_exp)


def solution(mesh):
    return jax.shard_map(
        functools.partial(per_device, mesh.shape["ep"], mesh.shape["grp"]),
        mesh=mesh,
        in_specs=(
            P(("ep", "grp"), None),
            P(("ep", "grp"), None),
            P(("ep", "grp"), None),
            P(None, "ep"),
            P(None, "ep"),
            P("ep", None),
            P(),
        ),
        out_specs=(P(("ep", "grp"), None), P()),
        check_vma=False,
    )
```

time: 56.6 us -> 37.3 us (0.66)
  blocking collectives: 37.5 us -> 0 us
  Pallas kernels: 0 us -> 26.4 us
  matrix products: 9.9 us -> 0 us
  local copies, waits for them, and re-layouts: 1 us -> 9.69 us
  other arithmetic: 3.71 us -> 0 us
  starting transfers between devices: 3.47 us -> 0 us
    pallas_call x0 -> x2, Pallas kernels: none -> 26.4 us  [the longest x1 22.8 us: per_device(): pl.pallas_call(functools.partial(exchange, n_ep, n_grp, n_exp, cap), out_...]
    psum x2 -> x0, blocking collectives: 24 us -> none  [the longest x1 13.6 us: count_loads(): return lax.psum(within, 'grp')]
    all_to_all x1 -> x0, blocking collectives: 13.5 us -> none  [per_device(): lax.all_to_all(outgoing, 'ep', split_axis=0, concat_axis=0, tiled=True)]
    dot_general x4 -> x0, matrix products: 9.9 us -> none  [the longest x1 4.74 us: per_device(): jnp.dot(hidden, w_down, preferred_element_type=jnp.float32)]
    unnamed x9 -> x18, local copies, waits for them, and re-layouts: 0.13 us -> 9.69 us
    all_to_all x1 -> x0, starting transfers between devices: 3.47 us -> none  [per_device(): lax.all_to_all(part.reshape(block.shape), 'ep', split_axis=0, concat_axis...]
    reduce_sum x3 -> x0, other arithmetic: 1.02 us -> none  [the longest x1 0.73 us: per_device(): select = jnp.sum(chosen.astype(jnp.float32), axis=2)]
    select_n x1 -> x0, other arithmetic: 0.87 us -> none  [per_device(): jnp.where(inside > 0, flat_ids * capacity + slot, win_experts * capacity)]
  transfers between devices with their start and end apart: 1 -> 0, of which waited for: 0 -> 0; matrix products, arithmetic and copies ran while one was open for 2% -> 0% of each run, Pallas kernels for 0% -> 0%
where the time goes in v1:
time: 37.3 us; the launch traced here: 36.8 us
  Pallas kernels  26.4 us (71%)
  local copies, waits for them, and re-layouts  9.69 us (26%)
  between operations  0.66 us (2%)
    pallas_call x1, Pallas kernels, per_device(): pl.pallas_call(functools.partial(exchange, n_ep, n_grp, n_exp, cap), out_...  22.8 us
    unnamed x18, local copies, waits for them, and re-layouts  9.69 us
    pallas_call x1, Pallas kernels, per_device(): pl.pallas_call(functools.partial(finish, mean), grid=(steps,), out_shape=...  3.59 us

profile of v1, /device:TPU:0, one launch (start us, length us, event | category | flops | bytes accessed | tf_op | source)
XLA Modules:
  0.0 36.8 jit_solution(1107973597840744828)
XLA Ops:
  0.6 0.0 copy-start
  0.6 1.7 %copy-done = bf16[4096,320]{0,1:T(8,128)(2,1)S(1)} copy-done((bf16[4096,320]{0,1:T(8,128)(2,1)S(1)}, bf16[4096,320]{0,1:T(8,128)(2,1)}, u32[]{:S(2)}) %copy-start) | copy-done | bytes 2621464
  2.4 0.0 copy-start.1
  2.4 1.7 %copy-done.1 = bf16[4096,320]{0,1:T(8,128)(2,1)S(1)} copy-done((bf16[4096,320]{0,1:T(8,128)(2,1)S(1)}, bf16[4096,320]{0,1:T(8,128)(2,1)}, u32[]{:S(2)}) %copy-start.1) | copy-done | bytes 2621464
  4.1 0.0 copy-start.2
  4.1 1.7 %copy-done.2 = bf16[320,4096]{1,0:T(8,128)(2,1)S(1)} copy-done((bf16[320,4096]{1,0:T(8,128)(2,1)S(1)}, bf16[320,4096]{1,0:T(8,128)(2,1)}, u32[]{:S(2)}) %copy-start.2) | copy-done | bytes 2621464
  5.9 0.0 copy-start.3
  5.9 1.2 %copy-done.3 = bf16[128,4096]{1,0:T(8,128)(2,1)S(1)} copy-done((bf16[128,4096]{1,0:T(8,128)(2,1)S(1)}, bf16[128,4096]{1,0:T(8,128)(2,1)}, u32[]{:S(2)}) %copy-start.3) | copy-done | bytes 1048600
  7.1 0.0 copy-start.6
  7.1 0.7 %copy-done.6 = s32[128,8]{0,1:T(8,128)S(1)} copy-done((s32[128,8]{0,1:T(8,128)S(1)}, s32[128,8]{0,1:T(8,128)}, u32[]{:S(2)}) %copy-start.6) | copy-done | bytes 4120
  7.8 0.0 copy-start.7
  7.8 0.7 %copy-done.7 = f32[128,8]{0,1:T(8,128)S(1)} copy-done((f32[128,8]{0,1:T(8,128)S(1)}, f32[128,8]{0,1:T(8,128)}, u32[]{:S(2)}) %copy-start.7) | copy-done | bytes 4120
  8.5 22.8 %exchange.1 = (bf16[32,4096]{1,0:T(8,128)(2,1)S(1)}, bf16[32,128]{1,0:T(8,128)(2,1)S(1)}, f32[8,128]{1,0:T(8,128)S(1)}) custom-call(bf16[128,4096]{1,0:T(8,128)(2,1)S(1)} %copy-done.3, s32[8,128]{1,0:T(8,128)S(1)} %bitcast.8, f32[8,128]{1,0:T(8,128)S(1)} %bitcast.9, bf16[320,4096]{1,0:T(8,128)(2,1)S(1)} %bitcast.6, bf16[320,4096]{1,0:T(8,128)(2,1)S(1)} %bitcast.7, ...), custom_call_target="tpu_custom_call" | custom-call | tf_op jit(solution)/shard_map/exchange/pallas_call | solution.py:191
  31.3 0.0 copy-start.4
  31.3 0.7 %copy-done.4 = bf16[32,4096]{1,0:T(8,128)(2,1)} copy-done((bf16[32,4096]{1,0:T(8,128)(2,1)}, bf16[32,4096]{1,0:T(8,128)(2,1)S(1)}, u32[]{:S(2)}) %copy-start.4) | copy-done | bytes 262168
  32.0 0.0 copy-start.5
  32.0 0.6 %copy-done.5 = bf16[32,128]{1,0:T(8,128)(2,1)} copy-done((bf16[32,128]{1,0:T(8,128)(2,1)}, bf16[32,128]{1,0:T(8,128)(2,1)S(1)}, u32[]{:S(2)}) %copy-start.5) | copy-done | bytes 8216
  32.6 0.0 copy-start.8
  32.6 0.6 %copy-done.8 = f32[8,128]{1,0:T(8,128)} copy-done((f32[8,128]{1,0:T(8,128)}, f32[8,128]{1,0:T(8,128)S(1)}, u32[]{:S(2)}) %copy-start.8) | copy-done | bytes 4120
  33.2 3.6 %finish.1 = (bf16[128,4096]{1,0:T(8,128)(2,1)}, f32[1,128]{1,0:T(1,128)}) custom-call(bf16[32,4096]{1,0:T(8,128)(2,1)} %copy-done.4, bf16[32,128]{1,0:T(8,128)(2,1)} %copy-done.5, f32[8,128]{1,0:T(8,128)} %copy-done.8, f32[1,128]{1,0:T(1,128)} %bitcast.10), custom_call_target="tpu_custom_call" | custom-call | tf_op jit(solution)/shard_map/finish/pallas_call | solution.py:227
Async XLA Ops:
  0.6 1.7 %copy-start = (bf16[4096,320]{0,1:T(8,128)(2,1)S(1)}, bf16[4096,320]{0,1:T(8,128)(2,1)}, u32[]{:S(2)}) copy-start(bf16[4096,320]{0,1:T(8,128)(2,1)} %param.10) | copy-start | bytes 7864324
  2.4 1.7 %copy-start.1 = (bf16[4096,320]{0,1:T(8,128)(2,1)S(1)}, bf16[4096,320]{0,1:T(8,128)(2,1)}, u32[]{:S(2)}) copy-start(bf16[4096,320]{0,1:T(8,128)(2,1)} %param.11) | copy-start | bytes 7864324
  4.1 1.7 %copy-start.2 = (bf16[320,4096]{1,0:T(8,128)(2,1)S(1)}, bf16[320,4096]{1,0:T(8,128)(2,1)}, u32[]{:S(2)}) copy-start(bf16[320,4096]{1,0:T(8,128)(2,1)} %wd_hbm.1) | copy-start | bytes 7864324
  5.9 1.2 %copy-start.3 = (bf16[128,4096]{1,0:T(8,128)(2,1)S(1)}, bf16[128,4096]{1,0:T(8,128)(2,1)}, u32[]{:S(2)}) copy-start(bf16[128,4096]{1,0:T(8,128)(2,1)} %tok_hbm.1) | copy-start | bytes 3145732
  7.1 0.7 %copy-start.6 = (s32[128,8]{0,1:T(8,128)S(1)}, s32[128,8]{0,1:T(8,128)}, u32[]{:S(2)}) copy-start(s32[128,8]{0,1:T(8,128)} %param.8) | copy-start | bytes 12292
  7.8 0.7 %copy-start.7 = (f32[128,8]{0,1:T(8,128)S(1)}, f32[128,8]{0,1:T(8,128)}, u32[]{:S(2)}) copy-start(f32[128,8]{0,1:T(8,128)} %param.9) | copy-start | bytes 12292
  31.3 0.7 %copy-start.4 = (bf16[32,4096]{1,0:T(8,128)(2,1)}, bf16[32,4096]{1,0:T(8,128)(2,1)S(1)}, u32[]{:S(2)}) copy-start(bf16[32,4096]{1,0:T(8,128)(2,1)S(1)} %get-tuple-element.7.scaled_ref) | copy-start | bytes 786436
  32.0 0.6 %copy-start.5 = (bf16[32,128]{1,0:T(8,128)(2,1)}, bf16[32,128]{1,0:T(8,128)(2,1)S(1)}, u32[]{:S(2)}) copy-start(bf16[32,128]{1,0:T(8,128)(2,1)S(1)} %get-tuple-element.8.sel_ref) | copy-start | bytes 24580
  32.6 0.6 %copy-start.8 = (f32[8,128]{1,0:T(8,128)}, f32[8,128]{1,0:T(8,128)S(1)}, u32[]{:S(2)}) copy-start(f32[8,128]{1,0:T(8,128)S(1)} %get-tuple-element.9.load_ref) | copy-start | bytes 12292

commit v2 on v1

--- a/solution.py
+++ b/solution.py
@@ -9,7 +9,7 @@
 
 SPLIT = 4
 MESH = pl.DeviceIdType.MESH
-ANY = pl.BlockSpec(memory_space=pl.ANY)
+HBM = pl.BlockSpec(memory_space=pltpu.HBM)
 VMEM = pl.BlockSpec(memory_space=pltpu.VMEM)
 F32 = jnp.float32
 BF16 = jnp.bfloat16
@@ -175,9 +175,18 @@
             copy.wait_send()
 
 
-def finish(mean, scaled_ref, sel_ref, load_ref, bias_ref, mixed_ref, new_ref):
-    mixed_ref[...] = lax.dot_general(sel_ref[...], scaled_ref[...], TN, preferred_element_type=F32).astype(BF16)
+def finish(mean, scaled_ref, sel_ref, load_ref, bias_ref, mixed_hbm, new_ref, tile, sem):
+    steps, _, size = tile.shape
+    copies = []
+    for c in range(steps):
+        cols = pl.ds(c * size, size)
+        tile[c] = lax.dot_general(sel_ref[...], scaled_ref[:, cols], TN, preferred_element_type=F32).astype(BF16)
+        copy = pltpu.make_async_copy(tile.at[c], mixed_hbm.at[:, cols], sem.at[c])
+        copy.start()
+        copies.append(copy)
     new_ref[...] = bias_ref[...] - 0.05 * (load_ref[:1, :] - mean) / jnp.sqrt(jnp.full((1, 1), mean, F32))
+    for copy in copies:
+        copy.wait()
 
 
 def per_device(n_ep, n_grp, tokens, expert_ids, combine, w_gate, w_up, w_down, bias):
@@ -191,11 +200,11 @@
     scaled, sel, load = pl.pallas_call(
         functools.partial(exchange, n_ep, n_grp, n_exp, cap),
         out_shape=(
-            jax.ShapeDtypeStruct((2 * slots, width), BF16),
-            jax.ShapeDtypeStruct((2 * slots, rows), BF16),
-            jax.ShapeDtypeStruct((8, n_exp), F32),
+            pltpu.VMEM((2 * slots, width), BF16),
+            pltpu.VMEM((2 * slots, rows), BF16),
+            pltpu.VMEM((8, n_exp), F32),
         ),
-        in_specs=[ANY] * 6,
+        in_specs=[HBM] * 6,
         out_specs=(VMEM, VMEM, VMEM),
         scratch_shapes=[
             pltpu.VMEM((rows, width), BF16),
@@ -219,22 +228,17 @@
             pltpu.SemaphoreType.DMA((n_ep + n_grp,)),
         ],
         compiler_params=pltpu.CompilerParams(
-            collective_id=0, has_side_effects=True, vmem_limit_bytes=40 * 1024 * 1024),
+            collective_id=0, has_side_effects=True, vmem_limit_bytes=56 * 1024 * 1024),
         name="exchange",
     )(tokens, expert_ids.T, combine.T, w_gate.T, w_up.T, w_down)
     steps = 4
-    tile = width // steps
     mixed, new_bias = pl.pallas_call(
         functools.partial(finish, mean),
-        grid=(steps,),
         out_shape=(jax.ShapeDtypeStruct((rows, width), BF16), jax.ShapeDtypeStruct((1, n_exp), F32)),
-        in_specs=[
-            pl.BlockSpec((2 * slots, tile), lambda i: (0, i)),
-            pl.BlockSpec((2 * slots, rows), lambda i: (0, 0)),
-            pl.BlockSpec((8, n_exp), lambda i: (0, 0)),
-            pl.BlockSpec((1, n_exp), lambda i: (0, 0)),
-        ],
-        out_specs=(pl.BlockSpec((rows, tile), lambda i: (0, i)), pl.BlockSpec((1, n_exp), lambda i: (0, 0))),
+        in_specs=[VMEM] * 4,
+        out_specs=(HBM, VMEM),
+        scratch_shapes=[pltpu.VMEM((steps, rows, width // steps), BF16), pltpu.SemaphoreType.DMA((steps,))],
+        compiler_params=pltpu.CompilerParams(vmem_limit_bytes=16 * 1024 * 1024),
         name="finish",
     )(scaled, sel, load, bias.reshape(1, n_exp))
     return mixed, new_bias.reshape(n_exp)

time: 37.3 us -> 25.8 us (0.69)
  local copies, waits for them, and re-layouts: 9.69 us -> 0.01 us
  Pallas kernels: 26.4 us -> 24.9 us
    unnamed x18 -> x2, local copies, waits for them, and re-layouts: 9.69 us -> 0.01 us
    pallas_call x1, Pallas kernels: 3.59 us -> 1.76 us  [per_device(): pl.pallas_call(functools.partial(finish, mean), out_shape=(jax.ShapeDtype...]
where the time goes in v2:
time: 25.8 us; the launch traced here: 25.6 us
  Pallas kernels  24.9 us (97%)
  between operations  0.66 us (3%)
    pallas_call x1, Pallas kernels, per_device(): pl.pallas_call(functools.partial(exchange, n_ep, n_grp, n_exp, cap), out_...  23.2 us
    pallas_call x1, Pallas kernels, per_device(): pl.pallas_call(functools.partial(finish, mean), out_shape=(jax.ShapeDtype...  1.76 us

profile of v2, /device:TPU:0, one launch (start us, length us, event | category | flops | bytes accessed | tf_op | source)
XLA Modules:
  0.0 25.6 jit_solution(13909329562387216211)
XLA Ops:
  0.6 0.0 copy-start
  0.6 23.2 %exchange.1 = (bf16[32,4096]{1,0:T(8,128)(2,1)S(1)}, bf16[32,128]{1,0:T(8,128)(2,1)S(1)}, f32[8,128]{1,0:T(8,128)S(1)}) custom-call(bf16[128,4096]{1,0:T(8,128)(2,1)} %tok_hbm.1, s32[8,128]{1,0:T(8,128)} %bitcast.9, f32[8,128]{1,0:T(8,128)} %bitcast.10, bf16[320,4096]{1,0:T(8,128)(2,1)} %bitcast.7, bf16[320,4096]{1,0:T(8,128)(2,1)} %bitcast.8, ...), custom_call_target="tpu_custom_call" | custom-call | tf_op jit(solution)/shard_map/exchange/pallas_call | solution.py:200
  23.8 0.0 copy-done
  23.8 1.8 %finish.1 = (bf16[128,4096]{1,0:T(8,128)(2,1)}, f32[1,128]{1,0:T(1,128)}) custom-call(bf16[32,4096]{1,0:T(8,128)(2,1)S(1)} %get-tuple-element.7.scaled_ref, bf16[32,128]{1,0:T(8,128)(2,1)S(1)} %get-tuple-element.8.sel_ref, f32[8,128]{1,0:T(8,128)S(1)} %get-tuple-element.9.load_ref, f32[1,128]{1,0:T(1,128)S(1)} %bitcast.6), custom_call_target="tpu_custom_call" | custom-call | tf_op jit(solution)/shard_map/finish/pallas_call | solution.py:235
Async XLA Ops:
  0.6 23.2 %copy-start = (f32[128]{0:T(128)S(1)}, f32[128]{0:T(128)}, u32[]{:S(2)}) copy-start(f32[128]{0:T(128)} %param.13) | copy-start | bytes 1540
